TPU v7x, 128 devices: a whole 4x4x4 slice. The times are simulated.
128 devices in a mesh: ep: 4 (over y_lo, core), fsdp: 32 (over z, y_hi, x).
Axes of the slice: x: 4, y: 4 (y_hi: 2, y_lo: 2; y = y_hi * 2 + y_lo), z: 4, core: 2. Of those that a mesh axis runs over, the one named last changes fastest.
Arguments:
- master_down: float32 [16, 6400, 4096], P('ep', None, 'fsdp'), may hold values from -0.15625 to 0.15625
- second_down: bfloat16 [16, 6400, 4096], P('ep', None, 'fsdp'), may hold values from -0.0390625 to 0.0390625
- router_weight: float32 [4096, 16], P('fsdp', 'ep'), may hold values from -0.09375 to 0.09375
- router_gain: float32 [4096], P('fsdp'), may hold values from 0.25 to 1.75
Outputs:
- final_down: bfloat16 [16, 6400, 4096], P('ep', 'fsdp')
- scale_down: float32 [16, 6400], P('ep', 'fsdp')
- serve_router: bfloat16 [4096, 16], replicated
All inputs are finite; a program needn't handle non-finite values.
Results may differ from a plain program's by a relative error of at most 0.001.
Values may be sent and summed in bfloat16 or wider, within the bound.
A program may use at most 128 MiB of HBM per device.

v0:
```python
import jax
import jax.numpy as jnp
from jax import lax
from jax.sharding import PartitionSpec as P


def rows_for(lines, count):
    spare = -len(lines) % count
    return jnp.pad(lines, [(0, spare)] + [(0, 0)] * (lines.ndim - 1))


def copy_for_each(value, axis):
    copies = jnp.broadcast_to(value, (lax.axis_size(axis), *value.shape))
    return lax.all_to_all(copies, axis, split_axis=0, concat_axis=0, tiled=True)


def laid_out(parts, dim):
    lengths = list(parts.shape[1:])
    lengths[dim] *= parts.shape[0]
    return jnp.moveaxis(parts, 0, dim).reshape(lengths)


def gathered_copies(value, axis, dim):
    parts = copy_for_each(value, axis)
    return laid_out(parts, dim)


def cut_along(value, dim, count):
    lengths = value.shape
    parts = value.reshape(*lengths[:dim], count, lengths[dim] // count, *lengths[dim + 1 :])
    return jnp.moveaxis(parts, dim, 0)


def summed_on_arrival(value, axis, dim):
    count = lax.axis_size(axis)
    parts = lax.all_to_all(cut_along(value, dim, count), axis, 0, 0, tiled=True)
    return jnp.sum(parts, axis=0)


def nested_sum(value, axes):
    lines = value.reshape(-1)
    padded = rows_for(lines, lax.axis_size(axes))
    whole = gathered_copies(summed_on_arrival(padded, axes, 0), axes, 0)
    return lax.slice_in_dim(whole, 0, len(lines)).reshape(value.shape)


def piece_ends(length, count):
    step = length // count
    if step >= 8:
        step -= step % 8
    return [step * k for k in range(1, count)]


def cut_exchange(value, axis, pieces, split_dim, concat_dim):
    parts = cut_along(value, split_dim, lax.axis_size(axis))
    split_at = max(range(1, max(2, parts.ndim - 1)), key=lambda d: parts.shape[d])
    finished = []
    for slab in jnp.split(parts, piece_ends(parts.shape[split_at], pieces), axis=split_at):
        if slab.size:
            finished.append(lax.all_to_all(slab, axis, split_axis=0, concat_axis=0, tiled=True))
    return laid_out(jnp.concatenate(finished, axis=split_at), concat_dim)


def shards(master_down, second_down, router_weight, router_gain):
    merged_down = master_down + second_down.astype(jnp.float32)
    total_down = nested_sum(jnp.sum(merged_down * merged_down, axis=2), "fsdp")
    scale_down = jnp.sqrt(total_down)
    narrow_down = (merged_down / jnp.expand_dims(scale_down, 2)).astype(jnp.bfloat16)
    final_down = cut_exchange(narrow_down, "fsdp", 2, 1, 2)
    scale_down = lax.dynamic_slice_in_dim(
        scale_down, lax.axis_index("fsdp") * final_down.shape[1], final_down.shape[1], axis=1
    )
    part_router = (router_weight * router_gain[:, None]).astype(jnp.bfloat16)
    row_router = gathered_copies(part_router, "fsdp", 0)
    serve_router = gathered_copies(row_router, "ep", 1)
    return (final_down, scale_down, serve_router)


def solution(mesh):
    return jax.shard_map(
        shards,
        mesh=mesh,
        in_specs=(P("ep", None, "fsdp"), P("ep", None, "fsdp"), P("fsdp", "ep"), P("fsdp")),
        out_specs=(P("ep", "fsdp", None), P("ep", "fsdp"), P()),
        check_vma=False,
    )
```

profile of v0, /device:TPU:0, one launch (start us, length us, event | category | flops | bytes accessed | tf_op | source)
XLA Modules:
  0.0 189.1 jit_solution(14402571469509063080)
XLA Ops:
  0.7 8.3 %multiply_reduce_fusion = f32[4,6400]{1,0:T(4,128)S(1)} fusion(f32[4,6400,128]{2,1,0:T(8,128)} %param.4, bf16[4,6400,128]{2,1,0:T(8,128)(2,1)} %param.5), kind=kLoop, calls=%fused_computation.1 | loop fusion | flops 13081600 | bytes 19763200 | tf_op jit(solution)/shard_map/reduce_sum | solution.py:66
  9.0 0.9 all_to_all.22
  9.9 10.9 %all-to-all-start = ((f32[32,1,800]{2,1,0:T(1,128)}), f32[32,1,800]{2,1,0:T(1,128)S(1)}, u32[]{:S(2)}, u32[]{:S(2)}) async-start(f32[32,1,800]{2,1,0:T(1,128)} %all_to_all.22), calls=%async_computation | async-start | bytes 229376 | tf_op jit(solution)/shard_map/all_to_all | solution.py:36
  20.8 10.2 %all-to-all-done = f32[32,1,800]{2,1,0:T(1,128)S(1)} async-done(((f32[32,1,800]{2,1,0:T(1,128)}), f32[32,1,800]{2,1,0:T(1,128)S(1)}, u32[]{:S(2)}, u32[]{:S(2)}) %all-to-all-start) | async-done | bytes 102432 | tf_op jit(solution)/shard_map/all_to_all | solution.py:36
  31.0 0.6 broadcast_in_dim.12
  31.6 3.9 %all-to-all-start.4 = ((bf16[32,128,4]{1,2,0:T(4,128)(2,1)}), bf16[32,128,4]{1,2,0:T(4,128)(2,1)S(1)}, u32[]{:S(2)}, u32[]{:S(2)}) async-start(bf16[32,128,4]{1,2,0:T(4,128)(2,1)} %broadcast_in_dim.12), calls=%async_computation.4 | async-start | bytes 65536 | tf_op jit(solution)/shard_map/all_to_all | solution.py:14
  35.5 9.8 %all-to-all-done.4 = bf16[32,128,4]{1,2,0:T(4,128)(2,1)S(1)} async-done(((bf16[32,128,4]{1,2,0:T(4,128)(2,1)}), bf16[32,128,4]{1,2,0:T(4,128)(2,1)S(1)}, u32[]{:S(2)}, u32[]{:S(2)}) %all-to-all-start.4) | async-done | bytes 32800 | tf_op jit(solution)/shard_map/all_to_all | solution.py:14
  45.4 13.5 %all_to_all.35 = f32[32,1,800]{2,1,0:T(1,128)S(1)} all-to-all(f32[32,1,800]{2,1,0:T(1,128)S(1)} %broadcast_in_dim.11), channel_id=1, replica_groups=mesh['ep'=4,'fsdp'=32] {'fsdp'}, dimensions={0} | all-to-all | bytes 204800 | tf_op jit(solution)/shard_map/all_to_all | solution.py:14
  58.9 0.7 broadcast_in_dim.13
  59.6 3.3 %all-to-all-start.5 = ((bf16[4,4096,4]{1,2,0:T(4,128)(2,1)}), bf16[4,4096,4]{1,2,0:T(4,128)(2,1)S(1)}, u32[]{:S(2)}, u32[]{:S(2)}) async-start(bf16[4,4096,4]{1,2,0:T(4,128)(2,1)} %broadcast_in_dim.13), calls=%async_computation.5 | async-start | bytes 262144 | tf_op jit(solution)/shard_map/all_to_all | solution.py:14
  62.9 0.5 sqrt_reduce_fusion
  63.5 11.0 %divide_convert_fusion = bf16[4,6400,128]{2,1,0:T(8,128)(2,1)S(1)} fusion(f32[4,6400,128]{2,1,0:T(8,128)} %param.4, bf16[4,6400,128]{2,1,0:T(8,128)(2,1)} %param.5, f32[4,6400]{1,0:T(4,128)S(1)} %sqrt.11), kind=kLoop, calls=%fused_computation | loop fusion | flops 13107200 | bytes 26316800 | tf_op jit(solution)/shard_map/convert_element_type | solution.py:68
  74.6 2.8 %copy-done = bf16[4,6400,128]{2,1,0:T(8,128)(2,1)} copy-done((bf16[4,6400,128]{2,1,0:T(8,128)(2,1)}, bf16[4,6400,128]{2,1,0:T(8,128)(2,1)S(1)}, u32[]{:S(2)}) %copy-start) | copy-done | bytes 6553624
  77.7 2.1 %copy.8 = bf16[32,4,96,128]{3,2,1,0:T(8,128)(2,1)} copy(bf16[32,4,96,128]{3,2,0,1:T(8,128)(2,1)S(1)} %split.8) | data formatting | bytes 6291456 | tf_op jit(solution)/shard_map/split | solution.py:58
  79.7 4.1 %all-to-all-start.2 = ((bf16[32,4,96,128]{3,2,1,0:T(8,128)(2,1)}), bf16[32,4,96,128]{3,2,1,0:T(8,128)(2,1)S(1)}, u32[]{:S(2)}, u32[]{:S(2)}) async-start(bf16[32,4,96,128]{3,2,1,0:T(8,128)(2,1)} %copy.8), calls=%async_computation.2 | async-start | bytes 6291456 | tf_op jit(solution)/shard_map/all_to_all | solution.py:60
  83.8 2.2 %split.9 = bf16[32,4,104,128]{3,2,0,1:T(8,128)(2,1)S(1)} slice(bf16[32,4,200,128]{3,2,0,1:T(8,128)(2,1)} %bitcast.14), slice={[0:32], [0:4], [96:200], [0:128]} | slice | bytes 6815744 | tf_op jit(solution)/shard_map/split | solution.py:58
  86.1 2.0 %copy.9 = bf16[32,4,104,128]{3,2,1,0:T(8,128)(2,1)} copy(bf16[32,4,104,128]{3,2,0,1:T(8,128)(2,1)S(1)} %split.9) | data formatting | bytes 6815744 | tf_op jit(solution)/shard_map/split | solution.py:58
  88.1 39.9 %all-to-all-done.2 = bf16[32,4,96,128]{3,2,1,0:T(8,128)(2,1)S(1)} async-done(((bf16[32,4,96,128]{3,2,1,0:T(8,128)(2,1)}), bf16[32,4,96,128]{3,2,1,0:T(8,128)(2,1)S(1)}, u32[]{:S(2)}, u32[]{:S(2)}) %all-to-all-start.2) | async-done | bytes 3145760 | tf_op jit(solution)/shard_map/all_to_all | solution.py:60
  128.0 1.6 copy-done.1
  129.7 8.7 %all-to-all-start.3 = ((bf16[32,4,104,128]{3,2,1,0:T(8,128)(2,1)}), bf16[32,4,104,128]{3,2,1,0:T(8,128)(2,1)S(1)}, u32[]{:S(2)}, u32[]{:S(2)}) async-start(bf16[32,4,104,128]{3,2,1,0:T(8,128)(2,1)} %copy.9), calls=%async_computation.3 | async-start | bytes 6815744 | tf_op jit(solution)/shard_map/all_to_all | solution.py:60
  138.4 0.7 reshape.40
  139.1 1.4 constant_dynamic-slice_fusion
  140.5 42.9 %all-to-all-done.3 = bf16[32,4,104,128]{3,2,1,0:T(8,128)(2,1)S(1)} async-done(((bf16[32,4,104,128]{3,2,1,0:T(8,128)(2,1)}), bf16[32,4,104,128]{3,2,1,0:T(8,128)(2,1)S(1)}, u32[]{:S(2)}, u32[]{:S(2)}) %all-to-all-start.3) | async-done | bytes 3407904 | tf_op jit(solution)/shard_map/all_to_all | solution.py:60
  183.4 5.6 %copy_bitcast_fusion = bf16[4,200,4096]{2,1,0:T(8,128)(2,1)} fusion(bf16[32,4,104,128]{3,2,1,0:T(8,128)(2,1)S(1)} %all-to-all-done.3, bf16[32,4,96,128]{3,2,1,0:T(8,128)(2,1)} %copy-done.1), kind=kLoop, calls=%fused_computation.3 | loop fusion | flops 13107200 | bytes 13107200 | tf_op jit(solution)/shard_map/reshape | solution.py:20
  (14 shorter events, 0.6 us)
Async XLA Ops:
  0.6 20.1 %copy-start.4 = (f32[128]{0:T(128)S(1)}, f32[128]{0:T(128)}, u32[]{:S(2)}) copy-start(f32[128]{0:T(128)} %param.7) | copy-start | bytes 1540
  0.6 20.1 %copy-start.3 = (f32[128,4]{0,1:T(4,128)S(1)}, f32[128,4]{0,1:T(4,128)}, u32[]{:S(2)}) copy-start(f32[128,4]{0,1:T(4,128)} %param.6) | copy-start | bytes 6148
  9.9 21.1 %all-to-all-start = ((f32[32,1,800]{2,1,0:T(1,128)}), f32[32,1,800]{2,1,0:T(1,128)S(1)}, u32[]{:S(2)}, u32[]{:S(2)}) async-start(f32[32,1,800]{2,1,0:T(1,128)} %all_to_all.22), calls=%async_computation | async-start | bytes 229376 | tf_op jit(solution)/shard_map/all_to_all | solution.py:36
  31.6 13.7 %all-to-all-start.4 = ((bf16[32,128,4]{1,2,0:T(4,128)(2,1)}), bf16[32,128,4]{1,2,0:T(4,128)(2,1)S(1)}, u32[]{:S(2)}, u32[]{:S(2)}) async-start(bf16[32,128,4]{1,2,0:T(4,128)(2,1)} %broadcast_in_dim.12), calls=%async_computation.4 | async-start | bytes 65536 | tf_op jit(solution)/shard_map/all_to_all | solution.py:14
  59.6 20.1 %all-to-all-start.5 = ((bf16[4,4096,4]{1,2,0:T(4,128)(2,1)}), bf16[4,4096,4]{1,2,0:T(4,128)(2,1)S(1)}, u32[]{:S(2)}, u32[]{:S(2)}) async-start(bf16[4,4096,4]{1,2,0:T(4,128)(2,1)} %broadcast_in_dim.13), calls=%async_computation.5 | async-start | bytes 262144 | tf_op jit(solution)/shard_map/all_to_all | solution.py:14
  63.5 11.0 %copy-start.2 = (f32[4,6400]{1,0:T(4,128)}, f32[4,6400]{1,0:T(4,128)S(1)}, u32[]{:S(2)}) copy-start(f32[4,6400]{1,0:T(4,128)S(1)} %sqrt.11) | copy-start | bytes 307204
  74.6 2.8 %copy-start = (bf16[4,6400,128]{2,1,0:T(8,128)(2,1)}, bf16[4,6400,128]{2,1,0:T(8,128)(2,1)S(1)}, u32[]{:S(2)}) copy-start(bf16[4,6400,128]{2,1,0:T(8,128)(2,1)S(1)} %divide_convert_fusion) | copy-start | bytes 19660804
  79.7 48.3 %all-to-all-start.2 = ((bf16[32,4,96,128]{3,2,1,0:T(8,128)(2,1)}), bf16[32,4,96,128]{3,2,1,0:T(8,128)(2,1)S(1)}, u32[]{:S(2)}, u32[]{:S(2)}) async-start(bf16[32,4,96,128]{3,2,1,0:T(8,128)(2,1)} %copy.8), calls=%async_computation.2 | async-start | bytes 6291456 | tf_op jit(solution)/shard_map/all_to_all | solution.py:60
  128.0 1.7 copy-start.1
  129.7 53.7 %all-to-all-start.3 = ((bf16[32,4,104,128]{3,2,1,0:T(8,128)(2,1)}), bf16[32,4,104,128]{3,2,1,0:T(8,128)(2,1)S(1)}, u32[]{:S(2)}, u32[]{:S(2)}) async-start(bf16[32,4,104,128]{3,2,1,0:T(8,128)(2,1)} %copy.9), calls=%async_computation.3 | async-start | bytes 6815744 | tf_op jit(solution)/shard_map/all_to_all | solution.py:60
where the time goes:
time: 193 us; the launch traced here: 189 us
  waiting for transfers between devices  103 us (53%)
  starting transfers between devices  30.9 us (16%)
  other arithmetic  25.1 us (13%)
  local copies, waits for them, and re-layouts  15.9 us (8%)
  blocking collectives  13.5 us (7%)
    all_to_all x2, waiting for transfers between devices, cut_exchange(): lax.all_to_all(slab, axis, split_axis=0, concat_axis=0, tiled=True)  82.9 us
    all_to_all x1, blocking collectives, copy_for_each(): return lax.all_to_all(copies, axis, split_axis=0, concat_axis=0, tiled=True)  13.5 us
    all_to_all x2, starting transfers between devices, cut_exchange(): lax.all_to_all(slab, axis, split_axis=0, concat_axis=0, tiled=True)  12.8 us
    convert_element_type x1, other arithmetic, shards(): (merged_down / jnp.expand_dims(scale_down, 2)).astype(jnp.bfloat16)  11 us
    all_to_all x1, starting transfers between devices, summed_on_arrival(): parts = lax.all_to_all(cut_along(value, dim, count), axis, 0, 0, tiled=True)  10.9 us
    all_to_all x1, waiting for transfers between devices, summed_on_arrival(): parts = lax.all_to_all(cut_along(value, dim, count), axis, 0, 0, tiled=True)  10.2 us
    all_to_all x2, waiting for transfers between devices, copy_for_each(): return lax.all_to_all(copies, axis, split_axis=0, concat_axis=0, tiled=True)  9.8 us
    reduce_sum x1, other arithmetic, shards(): total_down = nested_sum(jnp.sum(merged_down * merged_down, axis=2), 'fsdp')  8.33 us
  transfers between devices with their start and end apart: 5, of which 4 were waited for; matrix products, arithmetic and copies ran while one was open for 11% of the time, Pallas kernels for 0%

commit v1 on v0

v1 whole, which is shorter than its diff:
```python
import functools

import jax
import jax.numpy as jnp
from jax import lax
from jax.experimental import pallas as pl
from jax.experimental.pallas import tpu as pltpu
from jax.sharding import PartitionSpec as P

MESH = pl.DeviceIdType.MESH

SIZES = {"z": 4, "y": 2, "x": 4}
STRIDES = {"z": 8, "y": 4, "x": 1}
GROUP = 32
EXPERTS = 4
TILES = 25

PARTS = (("xyz", 0, 9), ("yzx", 9, 8), ("zxy", 17, 8))


def coords(index):
    return {"z": index // 8, "y": (index // 4) % 2, "x": index % 4}


def moved(at, offset, sign):
    return sum(
        lax.rem(at[dim] + sign * offset[dim] + SIZES[dim], SIZES[dim]) * STRIDES[dim] for dim in "zyx"
    )


def along(dim, step):
    return {other: step if other == dim else 0 for other in "zyx"}


def packing_mask():
    lane = lax.broadcasted_iota(jnp.int32, (TILES, 8, 128), 2)
    row = lax.broadcasted_iota(jnp.int32, (TILES, 8, 128), 1)
    tile = lax.broadcasted_iota(jnp.int32, (TILES, 8, 128), 0)
    return lane == lax.rem(row, 4) * 32 + tile


def kernel(
    master,
    second,
    weight,
    gain,
    final,
    scale,
    serve,
    merged,
    change,
    buf0,
    buf1,
    buf2,
    sums_out,
    sums_in,
    inverse,
    scales,
    columns,
    load_sem,
    sums_send,
    sums_recv,
    inv_send,
    inv_recv,
    part_send,
    part_recv,
    ep_send,
    ep_recv,
    router_send,
    router_recv,
):
    bufs = (buf0, buf1, buf2)
    me = lax.axis_index("fsdp")
    ep = lax.axis_index("ep")
    at = coords(me)

    barrier = pltpu.get_barrier_semaphore()

    def greet(r, _):
        pl.semaphore_signal(
            barrier, inc=1, device_id={"fsdp": moved(at, coords(r), 1)}, device_id_type=MESH
        )
        return _

    lax.fori_loop(1, GROUP, greet, 0)
    for k in range(1, 4):
        pl.semaphore_signal(
            barrier, inc=1, device_id={"ep": lax.rem(ep + k, 4)}, device_id_type=MESH
        )

    def loads(e):
        return (
            pltpu.make_async_copy(master.at[e], merged.at[e], load_sem.at[0, e]),
            pltpu.make_async_copy(second.at[e], change.at[e], load_sem.at[1, e]),
        )

    for e in range(EXPERTS):
        for copy in loads(e):
            copy.start()

    columns[0] = weight[...] * gain[...]

    def add_up(e):
        for copy in loads(e):
            copy.wait()

        def one(r, _):
            rows = pl.ds(moved(at, coords(r), 1) * TILES, TILES)
            value = merged[e, rows] + change[e, rows].astype(jnp.float32)
            merged[e, rows] = value
            sums = jnp.sum(value * value, axis=2, keepdims=True)
            placed = jnp.sum(jnp.where(packing_mask(), sums, 0.0), axis=0)
            sums_out[e, r, 0:1] = jnp.sum(placed[0:4], axis=0, keepdims=True)
            sums_out[e, r, 1:2] = jnp.sum(placed[4:8], axis=0, keepdims=True)
            return _

        lax.fori_loop(0, GROUP, one, 0)

    def sums_copy(e, r):
        return pltpu.make_async_remote_copy(
            src_ref=sums_out.at[e, r],
            dst_ref=sums_in.at[e, r],
            send_sem=sums_send.at[e],
            recv_sem=sums_recv.at[e],
            device_id={"fsdp": moved(at, coords(r), 1)},
            device_id_type=MESH,
        )

    def inv_copy(e, r):
        return pltpu.make_async_remote_copy(
            src_ref=inverse.at[e, 0],
            dst_ref=inverse.at[e, r],
            send_sem=inv_send.at[e],
            recv_sem=inv_recv.at[e],
            device_id={"fsdp": moved(at, coords(r), 1)},
            device_id_type=MESH,
        )

    def start_all(copy, e):
        def one(r, _):
            copy(e, r).start()
            return _

        lax.fori_loop(1, GROUP, one, 0)

    def wait_bytes(ref, sem):
        pltpu.make_async_copy(ref, ref, sem).wait()

    def send_sums(e):
        sums_in[e, 0] = sums_out[e, 0]
        start_all(sums_copy, e)

    def send_inverse(e):
        wait_bytes(sums_in.at[e, pl.ds(1, GROUP - 1)], sums_recv.at[e])
        root = jnp.sqrt(jnp.sum(sums_in[e], axis=0))
        scales[e] = root
        inverse[e, 0] = 1.0 / root
        start_all(inv_copy, e)

    def normalise(e):
        wait_bytes(inverse.at[e, pl.ds(1, GROUP - 1)], inv_recv.at[e])

        def one(r, _):
            offset = coords(r)
            back = {dim: lax.rem(SIZES[dim] - offset[dim], SIZES[dim]) for dim in "zyx"}
            owner = sum(back[dim] * STRIDES[dim] for dim in "zyx")
            packed = inverse[e, owner]
            spread = jnp.concatenate(
                [jnp.broadcast_to(packed[i : i + 1], (4, 128)) for i in range(2)], axis=0
            )
            factor = jnp.sum(jnp.where(packing_mask(), spread[None], 0.0), axis=2, keepdims=True)
            rows = pl.ds(moved(at, offset, 1) * TILES, TILES)
            value = (merged[e, rows] * factor).astype(jnp.bfloat16)
            for buf, (order, first, count) in zip(bufs, PARTS):
                a, b, c = order
                one_slot = lax.rem(offset[a] + SIZES[a] - 1, SIZES[a])
                two_slot = lax.rem(offset[b] + SIZES[b] - 1, SIZES[b])
                buf[e, one_slot, two_slot, offset[c]] = value[first : first + count]
            return _

        lax.fori_loop(0, GROUP, one, 0)

    def first_copies(e, p):
        order, _, _ = PARTS[p]
        n = [SIZES[dim] for dim in order]
        return [
            pltpu.make_async_remote_copy(
                src_ref=bufs[p].at[e, k - 1, pl.ds(0, n[1])],
                dst_ref=bufs[p].at[e, n[0] - 1 + k, pl.ds(0, n[1])],
                send_sem=part_send.at[e, p, 0, k - 1],
                recv_sem=part_recv.at[e, p, 0, k - 1],
                device_id={"fsdp": moved(at, along(order[0], k), 1)},
                device_id_type=MESH,
            )
            for k in ((1, 3, 2) if n[0] == 4 else (1,))
        ]

    def second_copies(e, p):
        order, _, _ = PARTS[p]
        n = [SIZES[dim] for dim in order]
        return [
            pltpu.make_async_remote_copy(
                src_ref=bufs[p].at[e, pl.ds(n[0] - 1, n[0]), k - 1],
                dst_ref=bufs[p].at[e, pl.ds(n[0] - 1, n[0]), n[1] - 1 + k],
                send_sem=part_send.at[e, p, 1, k - 1],
                recv_sem=part_recv.at[e, p, 1, k - 1],
                device_id={"fsdp": moved(at, along(order[1], k), 1)},
                device_id_type=MESH,
            )
            for k in ((1, 3, 2) if n[1] == 4 else (1,))
        ]

    def column(order, i, j):
        offset = {order[0]: i, order[1]: j, order[2]: 0}
        return moved(at, offset, -1)

    def landing(e, p, col):
        _, first, count = PARTS[p]
        return final.at[e, pl.ds(first, count), :, pl.ds(pl.multiple_of(col * 128, 128), 128)]

    def send_third(e, p):
        order, _, _ = PARTS[p]
        n = [SIZES[dim] for dim in order]

        def one(i, k):
            a, b = i // n[1], lax.rem(i, n[1])
            pltpu.make_async_remote_copy(
                src_ref=bufs[p].at[e, n[0] - 1 + a, n[1] - 1 + b, k],
                dst_ref=landing(e, p, column(order, a, b)),
                send_sem=part_send.at[e, p, 2, 0],
                recv_sem=part_recv.at[e, p, 2, 0],
                device_id={"fsdp": moved(at, along(order[2], k), 1)},
                device_id_type=MESH,
            ).start()
            return k

        for k in (1, 3, 2) if n[2] == 4 else (1,):
            lax.fori_loop(0, n[0] * n[1], one, k)

        def keep(i, _):
            a, b = i // n[1], lax.rem(i, n[1])
            col = column(order, a, b)
            first, count = PARTS[p][1:]
            final[e, pl.ds(first, count), :, pl.ds(pl.multiple_of(col * 128, 128), 128)] = bufs[p][
                e, n[0] - 1 + a, n[1] - 1 + b, 0
            ]
            return _

        lax.fori_loop(0, n[0] * n[1], keep, 0)

    def third_bytes(e, p):
        order, first, count = PARTS[p]
        n = [SIZES[dim] for dim in order]
        return final.at[e, pl.ds(first, count), :, pl.ds(0, (n[2] - 1) * n[0] * n[1] * 128)]

    def stage(e, s):
        for p in range(3):
            if s == 0:
                for copy in first_copies(e, p):
                    copy.start()
            elif s == 1:
                for copy in first_copies(e, p):
                    copy.wait_recv()
                for copy in second_copies(e, p):
                    copy.start()
            else:
                for copy in second_copies(e, p):
                    copy.wait_recv()
                send_third(e, p)

    def ep_copy(k):
        return pltpu.make_async_remote_copy(
            src_ref=columns.at[0],
            dst_ref=columns.at[k],
            send_sem=ep_send.at[k],
            recv_sem=ep_recv.at[k],
            device_id={"ep": lax.rem(ep + k, 4)},
            device_id_type=MESH,
        )

    def router_ref():
        return serve.at[:, pl.ds(pl.multiple_of(me * 128, 128), 128)]

    def router_copy(_, r):
        return pltpu.make_async_remote_copy(
            src_ref=router_ref(),
            dst_ref=router_ref(),
            send_sem=router_send,
            recv_sem=router_recv,
            device_id={"fsdp": moved(at, coords(r), 1)},
            device_id_type=MESH,
        )

    def send_router():
        for k in range(1, 4):
            ep_copy(k).wait_recv()
        rows = jnp.concatenate([columns[lax.rem(ep + 4 - i, 4)] for i in range(4)], axis=0)
        serve[:, pl.ds(pl.multiple_of(me * 128, 128), 128)] = rows.astype(jnp.bfloat16)
        start_all(router_copy, 0)

    add_up(0)
    pl.semaphore_wait(barrier, GROUP - 1 + 3)
    send_sums(0)
    for k in range(1, 4):
        ep_copy(k).start()
    add_up(1)
    send_sums(1)
    send_inverse(0)
    add_up(2)
    send_sums(2)
    normalise(0)
    stage(0, 0)
    send_inverse(1)
    add_up(3)
    send_sums(3)
    normalise(1)
    stage(1, 0)
    stage(0, 1)
    send_inverse(2)
    normalise(2)
    stage(2, 0)
    stage(1, 1)
    stage(0, 2)
    send_inverse(3)
    normalise(3)
    stage(3, 0)
    send_router()
    stage(2, 1)
    stage(1, 2)

    def order_of(index):
        source = lax.broadcasted_iota(jnp.int32, (128, 256), 0)
        target = lax.broadcasted_iota(jnp.int32, (128, 256), 1)
        place = lax.rem(source, 32) * 8 + index * 4 + source // 32
        return jnp.where((place == target) & (lax.rem(source, 32) < TILES), 1.0, 0.0)

    in_rows = sum(
        jnp.dot(
            scales[:, index],
            order_of(index),
            precision=lax.Precision.HIGHEST,
            preferred_element_type=jnp.float32,
        )
        for index in range(2)
    )
    scale[...] = in_rows[:, 0 : TILES * 8]

    stage(3, 1)
    stage(2, 2)
    stage(3, 2)

    for e in range(EXPERTS):
        wait_bytes(sums_out.at[e, pl.ds(1, GROUP - 1)], sums_send.at[e])
        wait_bytes(inverse.at[e, pl.ds(1, GROUP - 1)], inv_send.at[e])
        for p in range(3):
            for copy in first_copies(e, p) + second_copies(e, p):
                copy.wait_send()
            wait_bytes(third_bytes(e, p), part_send.at[e, p, 2, 0])
            wait_bytes(third_bytes(e, p), part_recv.at[e, p, 2, 0])
    for k in range(1, 4):
        ep_copy(k).wait_send()
    others = serve.at[:, pl.ds(0, (GROUP - 1) * 128)]
    wait_bytes(others, router_send)
    wait_bytes(others, router_recv)


def exchange(master, second, weight, gain):
    vmem = pl.BlockSpec(memory_space=pltpu.VMEM)
    hbm = pl.BlockSpec(memory_space=pltpu.HBM)
    rows = EXPERTS, GROUP * TILES, 8, 128
    part_bufs = []
    for order, _, count in PARTS:
        a, b, c = (SIZES[dim] for dim in order)
        part_bufs.append(
            pltpu.VMEM((EXPERTS, 2 * a - 1, 2 * b - 1, c, count, 8, 128), jnp.bfloat16)
        )
    dma = pltpu.SemaphoreType.DMA
    return pl.pallas_call(
        kernel,
        name="exchange",
        out_shape=(
            jax.ShapeDtypeStruct((EXPERTS, TILES, 8, GROUP * 128), jnp.bfloat16),
            jax.ShapeDtypeStruct((EXPERTS, TILES * 8), jnp.float32),
            jax.ShapeDtypeStruct((16, GROUP * 128), jnp.bfloat16),
        ),
        in_specs=[hbm, hbm, vmem, vmem],
        out_specs=(vmem, vmem, vmem),
        scratch_shapes=[
            pltpu.VMEM(rows, jnp.float32),
            pltpu.VMEM(rows, jnp.bfloat16),
            *part_bufs,
            pltpu.VMEM((EXPERTS, GROUP, 2, 128), jnp.float32),
            pltpu.VMEM((EXPERTS, GROUP, 2, 128), jnp.float32),
            pltpu.VMEM((EXPERTS, GROUP, 2, 128), jnp.float32),
            pltpu.VMEM((EXPERTS, 2, 128), jnp.float32),
            pltpu.VMEM((4, 4, 128), jnp.float32),
            dma((2, EXPERTS)),
            dma((EXPERTS,)),
            dma((EXPERTS,)),
            dma((EXPERTS,)),
            dma((EXPERTS,)),
            dma((EXPERTS, 3, 3, 3)),
            dma((EXPERTS, 3, 3, 3)),
            dma((4,)),
            dma((4,)),
            dma(()),
            dma(()),
        ],
        compiler_params=pltpu.CompilerParams(
            collective_id=0, has_side_effects=True, vmem_limit_bytes=63 * 2**20
        ),
    )(
        master.reshape(rows),
        second.reshape(rows),
        weight.T,
        gain.reshape(1, 128),
    )


def shards(master_down, second_down, router_weight, router_gain):
    final, scale, serve = exchange(master_down, second_down, router_weight, router_gain)
    return final.reshape(EXPERTS, TILES * 8, GROUP * 128), scale, serve.T


def solution(mesh):
    return jax.shard_map(
        shards,
        mesh=mesh,
        in_specs=(P("ep", None, "fsdp"), P("ep", None, "fsdp"), P("fsdp", "ep"), P("fsdp")),
        out_specs=(P("ep", "fsdp", None), P("ep", "fsdp"), P()),
        check_vma=False,
    )
```

time: 193 us -> 136 us (0.70); the launches traced: 189 us -> 135 us
  Pallas kernels: 0 us -> 127 us
  waiting for transfers between devices: 103 us -> 0 us
  starting transfers between devices: 30.9 us -> 0 us
  other arithmetic: 25.1 us -> 0 us
  blocking collectives: 13.5 us -> 0 us
  local copies, waits for them, and re-layouts: 15.9 us -> 7.78 us
    pallas_call x0 -> x1, Pallas kernels: none -> 127 us  [exchange(): pl.pallas_call(kernel, name='exchange', out_shape=(jax.ShapeDtypeStruct((...]
    all_to_all x5 -> x0, waiting for transfers between devices: 103 us -> none  [the longest x2 82.9 us: cut_exchange(): lax.all_to_all(slab, axis, split_axis=0, concat_axis=0, tiled=True)]
    all_to_all x5 -> x0, starting transfers between devices: 30.9 us -> none  [the longest x2 12.8 us: cut_exchange(): lax.all_to_all(slab, axis, split_axis=0, concat_axis=0, tiled=True)]
    all_to_all x1 -> x0, blocking collectives: 13.5 us -> none  [copy_for_each(): return lax.all_to_all(copies, axis, split_axis=0, concat_axis=0, tiled=True)]
    convert_element_type x2 -> x0, other arithmetic: 11 us -> none  [the longest x1 11 us: shards(): (merged_down / jnp.expand_dims(scale_down, 2)).astype(jnp.bfloat16)]
    reduce_sum x2 -> x0, other arithmetic: 8.42 us -> none  [the longest x1 8.33 us: shards(): total_down = nested_sum(jnp.sum(merged_down * merged_down, axis=2), 'fsdp')]
    split x4 -> x0, local copies, waits for them, and re-layouts: 6.63 us -> none  [cut_exchange(): jnp.split(parts, piece_ends(parts.shape[split_at], pieces), axis=split_at)]
    reshape x1 -> x0, other arithmetic: 5.64 us -> none  [laid_out(): return jnp.moveaxis(parts, 0, dim).reshape(lengths)]
  transfers between devices with their start and end apart: 5 -> 0, of which waited for: 4 -> 0; matrix products, arithmetic and copies ran while one was open for 11% -> 0% of each run, Pallas kernels for 0% -> 0%
where the time goes in v1:
time: 136 us; the launch traced here: 135 us
  Pallas kernels  127 us (93%)
  local copies, waits for them, and re-layouts  7.78 us (6%)
    pallas_call x1, Pallas kernels, exchange(): pl.pallas_call(kernel, name='exchange', out_shape=(jax.ShapeDtypeStruct((...  127 us
    unnamed x7, local copies, waits for them, and re-layouts  7.78 us

profile of v1, /device:TPU:0, one launch (start us, length us, event | category | flops | bytes accessed | tf_op | source)
XLA Modules:
  0.0 135.5 jit_solution(2581728663368442681)
XLA Ops:
  0.6 127.0 %exchange.1 = (bf16[4,25,8,4096]{3,2,1,0:T(8,128)(2,1)}, f32[4,200]{1,0:T(4,128)}, bf16[16,4096]{1,0:T(8,128)(2,1)}) custom-call(f32[4,800,8,128]{3,2,1,0:T(8,128)} %bitcast.6, bf16[4,800,8,128]{3,2,1,0:T(8,128)(2,1)} %bitcast.7, f32[4,128]{1,0:T(4,128)} %bitcast.10, f32[1,128]{1,0:T(1,128)} %bitcast.11), custom_call_target="tpu_custom_call" | custom-call | tf_op jit(solution)/shard_map/exchange/pallas_call | solution.py:378
  127.7 0.0 copy-start.1
  127.7 0.0 copy-start
  127.7 6.5 %copy.10 = bf16[4,200,4096]{2,1,0:T(8,128)(2,1)} copy(bf16[4,200,4096]{2,1,0:T(8,128)(2,1)} %bitcast.8) | data formatting | bytes 13107200
  134.2 0.0 copy-done.1
  134.2 0.6 copy.11
  134.8 0.0 copy-done
  134.8 0.7 copy.12
Async XLA Ops:
  127.7 6.5 %copy-start.1 = (f32[4,200]{1,0:T(4,128)S(1)}, f32[4,200]{1,0:T(4,128)}, u32[]{:S(2)}) copy-start(f32[4,200]{1,0:T(4,128)} %get-tuple-element.13) | copy-start | bytes 9604
  127.7 7.1 %copy-start = (bf16[16,4096]{1,0:T(8,128)(2,1)S(1)}, bf16[16,4096]{1,0:T(8,128)(2,1)}, u32[]{:S(2)}) copy-start(bf16[16,4096]{1,0:T(8,128)(2,1)} %get-tuple-element.8) | copy-start | bytes 393220

commit v2 on v1

--- a/solution.py
+++ b/solution.py
@@ -14,6 +14,14 @@
 GROUP = 32
 EXPERTS = 4
 TILES = 25
+UNROLL = 4
+SUM_GROUPS = ((0,), (1, 2, 3))
+
+
+def place_of(e):
+    g = next(i for i, group in enumerate(SUM_GROUPS) if e in group)
+    return g, SUM_GROUPS[g].index(e)
+
 
 PARTS = (("xyz", 0, 9), ("yzx", 9, 8), ("zxy", 17, 8))
 
@@ -32,11 +40,10 @@
     return {other: step if other == dim else 0 for other in "zyx"}
 
 
-def packing_mask():
-    lane = lax.broadcasted_iota(jnp.int32, (TILES, 8, 128), 2)
-    row = lax.broadcasted_iota(jnp.int32, (TILES, 8, 128), 1)
-    tile = lax.broadcasted_iota(jnp.int32, (TILES, 8, 128), 0)
-    return lane == lax.rem(row, 4) * 32 + tile
+def places():
+    lane = lax.broadcasted_iota(jnp.int32, (8, 128), 1)
+    row = lax.broadcasted_iota(jnp.int32, (8, 128), 0)
+    return lane - lax.rem(row, 4) * 32
 
 
 def kernel(
@@ -52,9 +59,12 @@
     buf0,
     buf1,
     buf2,
-    sums_out,
-    sums_in,
-    inverse,
+    sums_out0,
+    sums_out1,
+    sums_in0,
+    sums_in1,
+    inverse0,
+    inverse1,
     scales,
     columns,
     load_sem,
@@ -70,6 +80,9 @@
     router_recv,
 ):
     bufs = (buf0, buf1, buf2)
+    sums_out = (sums_out0, sums_out1)
+    sums_in = (sums_in0, sums_in1)
+    inverse = (inverse0, inverse1)
     me = lax.axis_index("fsdp")
     ep = lax.axis_index("ep")
     at = coords(me)
@@ -100,45 +113,56 @@
 
     columns[0] = weight[...] * gain[...]
 
+    def merged_rows(e, index):
+        rows = pl.ds(index * TILES, TILES)
+        return merged[e, rows] + change[e, rows].astype(jnp.float32)
+
     def add_up(e):
         for copy in loads(e):
             copy.wait()
-
-        def one(r, _):
-            rows = pl.ds(moved(at, coords(r), 1) * TILES, TILES)
-            value = merged[e, rows] + change[e, rows].astype(jnp.float32)
-            merged[e, rows] = value
-            sums = jnp.sum(value * value, axis=2, keepdims=True)
-            placed = jnp.sum(jnp.where(packing_mask(), sums, 0.0), axis=0)
-            sums_out[e, r, 0:1] = jnp.sum(placed[0:4], axis=0, keepdims=True)
-            sums_out[e, r, 1:2] = jnp.sum(placed[4:8], axis=0, keepdims=True)
+        g, i = place_of(e)
+
+        def some(step, _):
+            key = places()
+            packed = []
+            for u in range(UNROLL):
+                value = merged_rows(e, moved(at, coords(step * UNROLL + u), 1))
+                sums = jnp.sum(value * value, axis=2, keepdims=True)
+                acc = jnp.zeros((8, 128), jnp.float32)
+                for j in range(TILES):
+                    acc = jnp.where(key == j, sums[j], acc)
+                packed.append(acc)
+            for u, acc in enumerate(packed):
+                r = step * UNROLL + u
+                sums_out[g][r, i, 0:1] = jnp.sum(acc[0:4], axis=0, keepdims=True)
+                sums_out[g][r, i, 1:2] = jnp.sum(acc[4:8], axis=0, keepdims=True)
             return _
 
-        lax.fori_loop(0, GROUP, one, 0)
-
-    def sums_copy(e, r):
+        lax.fori_loop(0, GROUP // UNROLL, some, 0)
+
+    def sums_copy(g, r):
         return pltpu.make_async_remote_copy(
-            src_ref=sums_out.at[e, r],
-            dst_ref=sums_in.at[e, r],
-            send_sem=sums_send.at[e],
-            recv_sem=sums_recv.at[e],
+            src_ref=sums_out[g].at[r],
+            dst_ref=sums_in[g].at[r],
+            send_sem=sums_send.at[g],
+            recv_sem=sums_recv.at[g],
             device_id={"fsdp": moved(at, coords(r), 1)},
             device_id_type=MESH,
         )
 
-    def inv_copy(e, r):
+    def inv_copy(g, r):
         return pltpu.make_async_remote_copy(
-            src_ref=inverse.at[e, 0],
-            dst_ref=inverse.at[e, r],
-            send_sem=inv_send.at[e],
-            recv_sem=inv_recv.at[e],
+            src_ref=inverse[g].at[0],
+            dst_ref=inverse[g].at[r],
+            send_sem=inv_send.at[g],
+            recv_sem=inv_recv.at[g],
             device_id={"fsdp": moved(at, coords(r), 1)},
             device_id_type=MESH,
         )
 
-    def start_all(copy, e):
+    def start_all(copy, g):
         def one(r, _):
-            copy(e, r).start()
+            copy(g, r).start()
             return _
 
         lax.fori_loop(1, GROUP, one, 0)
@@ -146,39 +170,52 @@
     def wait_bytes(ref, sem):
         pltpu.make_async_copy(ref, ref, sem).wait()
 
-    def send_sums(e):
-        sums_in[e, 0] = sums_out[e, 0]
-        start_all(sums_copy, e)
-
-    def send_inverse(e):
-        wait_bytes(sums_in.at[e, pl.ds(1, GROUP - 1)], sums_recv.at[e])
-        root = jnp.sqrt(jnp.sum(sums_in[e], axis=0))
-        scales[e] = root
-        inverse[e, 0] = 1.0 / root
-        start_all(inv_copy, e)
+    def others_of(ref):
+        return ref.at[pl.ds(1, GROUP - 1)]
+
+    def send_sums(g):
+        sums_in[g][0] = sums_out[g][0]
+        start_all(sums_copy, g)
+
+    def send_inverse(g):
+        wait_bytes(others_of(sums_in[g]), sums_recv.at[g])
+        for i, e in enumerate(SUM_GROUPS[g]):
+            root = jnp.sqrt(jnp.sum(sums_in[g][:, i], axis=0))
+            scales[e] = root
+            inverse[g][0, i] = 1.0 / root
+        start_all(inv_copy, g)
 
     def normalise(e):
-        wait_bytes(inverse.at[e, pl.ds(1, GROUP - 1)], inv_recv.at[e])
-
-        def one(r, _):
-            offset = coords(r)
-            back = {dim: lax.rem(SIZES[dim] - offset[dim], SIZES[dim]) for dim in "zyx"}
-            owner = sum(back[dim] * STRIDES[dim] for dim in "zyx")
-            packed = inverse[e, owner]
-            spread = jnp.concatenate(
-                [jnp.broadcast_to(packed[i : i + 1], (4, 128)) for i in range(2)], axis=0
-            )
-            factor = jnp.sum(jnp.where(packing_mask(), spread[None], 0.0), axis=2, keepdims=True)
-            rows = pl.ds(moved(at, offset, 1) * TILES, TILES)
-            value = (merged[e, rows] * factor).astype(jnp.bfloat16)
-            for buf, (order, first, count) in zip(bufs, PARTS):
-                a, b, c = order
-                one_slot = lax.rem(offset[a] + SIZES[a] - 1, SIZES[a])
-                two_slot = lax.rem(offset[b] + SIZES[b] - 1, SIZES[b])
-                buf[e, one_slot, two_slot, offset[c]] = value[first : first + count]
+        g, i = place_of(e)
+        if i == 0:
+            wait_bytes(others_of(inverse[g]), inv_recv.at[g])
+
+        def some(step, _):
+            key = places()
+            for u in range(UNROLL):
+                offset = coords(step * UNROLL + u)
+                back = {dim: lax.rem(SIZES[dim] - offset[dim], SIZES[dim]) for dim in "zyx"}
+                owner = sum(back[dim] * STRIDES[dim] for dim in "zyx")
+                packed = inverse[g][owner, i]
+                spread = jnp.concatenate(
+                    [jnp.broadcast_to(packed[h : h + 1], (4, 128)) for h in range(2)], axis=0
+                )
+                factor = jnp.stack(
+                    [
+                        jnp.sum(jnp.where(key == j, spread, 0.0), axis=1, keepdims=True)
+                        for j in range(TILES)
+                    ]
+                )
+                value = merged_rows(e, moved(at, offset, 1)) * factor
+                value = value.astype(jnp.bfloat16)
+                for buf, (order, first, count) in zip(bufs, PARTS):
+                    a, b, c = order
+                    one_slot = lax.rem(offset[a] + SIZES[a] - 1, SIZES[a])
+                    two_slot = lax.rem(offset[b] + SIZES[b] - 1, SIZES[b])
+                    buf[e, one_slot, two_slot, offset[c]] = value[first : first + count]
             return _
 
-        lax.fori_loop(0, GROUP, one, 0)
+        lax.fori_loop(0, GROUP // UNROLL, some, 0)
 
     def first_copies(e, p):
         order, _, _ = PARTS[p]
@@ -303,28 +340,23 @@
     send_sums(0)
     for k in range(1, 4):
         ep_copy(k).start()
-    add_up(1)
+    for e in SUM_GROUPS[1]:
+        add_up(e)
     send_sums(1)
     send_inverse(0)
-    add_up(2)
-    send_sums(2)
+    send_router()
     normalise(0)
     stage(0, 0)
     send_inverse(1)
-    add_up(3)
-    send_sums(3)
     normalise(1)
     stage(1, 0)
     stage(0, 1)
-    send_inverse(2)
     normalise(2)
     stage(2, 0)
     stage(1, 1)
     stage(0, 2)
-    send_inverse(3)
     normalise(3)
     stage(3, 0)
-    send_router()
     stage(2, 1)
     stage(1, 2)
 
@@ -349,9 +381,10 @@
     stage(2, 2)
     stage(3, 2)
 
+    for g in range(len(SUM_GROUPS)):
+        wait_bytes(others_of(sums_out[g]), sums_send.at[g])
+        wait_bytes(others_of(inverse[g]), inv_send.at[g])
     for e in range(EXPERTS):
-        wait_bytes(sums_out.at[e, pl.ds(1, GROUP - 1)], sums_send.at[e])
-        wait_bytes(inverse.at[e, pl.ds(1, GROUP - 1)], inv_send.at[e])
         for p in range(3):
             for copy in first_copies(e, p) + second_copies(e, p):
                 copy.wait_send()
@@ -389,16 +422,17 @@
             pltpu.VMEM(rows, jnp.float32),
             pltpu.VMEM(rows, jnp.bfloat16),
             *part_bufs,
-            pltpu.VMEM((EXPERTS, GROUP, 2, 128), jnp.float32),
-            pltpu.VMEM((EXPERTS, GROUP, 2, 128), jnp.float32),
-            pltpu.VMEM((EXPERTS, GROUP, 2, 128), jnp.float32),
+            *(
+                pltpu.VMEM((GROUP, len(group), 2, 128), jnp.float32)
+                for group in SUM_GROUPS + SUM_GROUPS + SUM_GROUPS
+            ),
             pltpu.VMEM((EXPERTS, 2, 128), jnp.float32),
             pltpu.VMEM((4, 4, 128), jnp.float32),
             dma((2, EXPERTS)),
-            dma((EXPERTS,)),
-            dma((EXPERTS,)),
-            dma((EXPERTS,)),
-            dma((EXPERTS,)),
+            dma((len(SUM_GROUPS),)),
+            dma((len(SUM_GROUPS),)),
+            dma((len(SUM_GROUPS),)),
+            dma((len(SUM_GROUPS),)),
             dma((EXPERTS, 3, 3, 3)),
             dma((EXPERTS, 3, 3, 3)),
             dma((4,)),

time: 136 us -> 119 us (0.88)
  Pallas kernels: 127 us -> 110 us
    pallas_call x1, Pallas kernels: 127 us -> 110 us  [exchange(): pl.pallas_call(kernel, name='exchange', out_shape=(jax.ShapeDtypeStruct((...]
where the time goes in v2:
time: 119 us
  Pallas kernels  110 us (92%)
  local copies, waits for them, and re-layouts  7.78 us (7%)
    pallas_call x1, Pallas kernels, exchange(): pl.pallas_call(kernel, name='exchange', out_shape=(jax.ShapeDtypeStruct((...  110 us
    unnamed x7, local copies, waits for them, and re-layouts  7.78 us

profile of v2, /device:TPU:0, one launch (start us, length us, event | category | flops | bytes accessed | tf_op | source)
XLA Modules:
  0.0 118.7 jit_solution(13210331628690532454)
XLA Ops:
  0.6 110.3 %exchange.1 = (bf16[4,25,8,4096]{3,2,1,0:T(8,128)(2,1)}, f32[4,200]{1,0:T(4,128)}, bf16[16,4096]{1,0:T(8,128)(2,1)}) custom-call(f32[4,800,8,128]{3,2,1,0:T(8,128)} %bitcast.6, bf16[4,800,8,128]{3,2,1,0:T(8,128)(2,1)} %bitcast.7, f32[4,128]{1,0:T(4,128)} %bitcast.10, f32[1,128]{1,0:T(1,128)} %bitcast.11), custom_call_target="tpu_custom_call" | custom-call | tf_op jit(solution)/shard_map/exchange/pallas_call | solution.py:411
  110.9 0.0 copy-start.1
  111.0 0.0 copy-start
  111.0 6.5 %copy.10 = bf16[4,200,4096]{2,1,0:T(8,128)(2,1)} copy(bf16[4,200,4096]{2,1,0:T(8,128)(2,1)} %bitcast.8) | data formatting | bytes 13107200
  117.5 0.0 copy-done.1
  117.5 0.6 copy.11
  118.1 0.0 copy-done
  118.1 0.7 copy.12
Async XLA Ops:
  110.9 6.5 %copy-start.1 = (f32[4,200]{1,0:T(4,128)S(1)}, f32[4,200]{1,0:T(4,128)}, u32[]{:S(2)}) copy-start(f32[4,200]{1,0:T(4,128)} %get-tuple-element.13) | copy-start | bytes 9604
  111.0 7.1 %copy-start = (bf16[16,4096]{1,0:T(8,128)(2,1)S(1)}, bf16[16,4096]{1,0:T(8,128)(2,1)}, u32[]{:S(2)}) copy-start(bf16[16,4096]{1,0:T(8,128)(2,1)} %get-tuple-element.8) | copy-start | bytes 393220

commit v3 on v2

--- a/solution.py
+++ b/solution.py
@@ -14,7 +14,7 @@
 GROUP = 32
 EXPERTS = 4
 TILES = 25
-UNROLL = 4
+UNROLL = 8
 SUM_GROUPS = ((0,), (1, 2, 3))
 
 
@@ -192,6 +192,7 @@
 
         def some(step, _):
             key = places()
+            factors = []
             for u in range(UNROLL):
                 offset = coords(step * UNROLL + u)
                 back = {dim: lax.rem(SIZES[dim] - offset[dim], SIZES[dim]) for dim in "zyx"}
@@ -200,13 +201,15 @@
                 spread = jnp.concatenate(
                     [jnp.broadcast_to(packed[h : h + 1], (4, 128)) for h in range(2)], axis=0
                 )
-                factor = jnp.stack(
+                factors.append(
                     [
                         jnp.sum(jnp.where(key == j, spread, 0.0), axis=1, keepdims=True)
                         for j in range(TILES)
                     ]
                 )
-                value = merged_rows(e, moved(at, offset, 1)) * factor
+            for u in range(UNROLL):
+                offset = coords(step * UNROLL + u)
+                value = merged_rows(e, moved(at, offset, 1)) * jnp.stack(factors[u])
                 value = value.astype(jnp.bfloat16)
                 for buf, (order, first, count) in zip(bufs, PARTS):
                     a, b, c = order
@@ -345,9 +348,9 @@
     send_sums(1)
     send_inverse(0)
     send_router()
+    send_inverse(1)
     normalise(0)
     stage(0, 0)
-    send_inverse(1)
     normalise(1)
     stage(1, 0)
     stage(0, 1)
@@ -412,9 +415,9 @@
         kernel,
         name="exchange",
         out_shape=(
-            jax.ShapeDtypeStruct((EXPERTS, TILES, 8, GROUP * 128), jnp.bfloat16),
-            jax.ShapeDtypeStruct((EXPERTS, TILES * 8), jnp.float32),
-            jax.ShapeDtypeStruct((16, GROUP * 128), jnp.bfloat16),
+            pltpu.VMEM((EXPERTS, TILES, 8, GROUP * 128), jnp.bfloat16),
+            pltpu.VMEM((EXPERTS, TILES * 8), jnp.float32),
+            pltpu.VMEM((16, GROUP * 128), jnp.bfloat16),
         ),
         in_specs=[hbm, hbm, vmem, vmem],
         out_specs=(vmem, vmem, vmem),
@@ -441,7 +444,7 @@
             dma(()),
         ],
         compiler_params=pltpu.CompilerParams(
-            collective_id=0, has_side_effects=True, vmem_limit_bytes=63 * 2**20
+            collective_id=0, has_side_effects=True, vmem_limit_bytes=48 * 2**20
         ),
     )(
         master.reshape(rows),
@@ -451,8 +454,38 @@
     )
 
 
+def write_out(final, scale, serve, final_out, scale_out, serve_out, sem):
+    copies = [
+        pltpu.make_async_copy(final.at[e], final_out.at[e], sem.at[e]) for e in range(EXPERTS)
+    ]
+    copies.append(pltpu.make_async_copy(serve, serve_out, sem.at[EXPERTS]))
+    copies.append(pltpu.make_async_copy(scale, scale_out, sem.at[EXPERTS + 1]))
+    for copy in copies:
+        copy.start()
+    for copy in copies:
+        copy.wait()
+
+
+def written(final, scale, serve):
+    vmem = pl.BlockSpec(memory_space=pltpu.VMEM)
+    hbm = pl.BlockSpec(memory_space=pltpu.HBM)
+    return pl.pallas_call(
+        write_out,
+        name="write_out",
+        out_shape=tuple(
+            jax.ShapeDtypeStruct(value.shape, value.dtype) for value in (final, scale, serve)
+        ),
+        in_specs=[vmem] * 3,
+        out_specs=(hbm,) * 3,
+        scratch_shapes=[pltpu.SemaphoreType.DMA((EXPERTS + 2,))],
+        compiler_params=pltpu.CompilerParams(vmem_limit_bytes=16 * 2**20),
+    )(final, scale, serve)
+
+
 def shards(master_down, second_down, router_weight, router_gain):
-    final, scale, serve = exchange(master_down, second_down, router_weight, router_gain)
+    final, scale, serve = written(
+        *exchange(master_down, second_down, router_weight, router_gain)
+    )
     return final.reshape(EXPERTS, TILES * 8, GROUP * 128), scale, serve.T
 
 

time: 119 us -> 102 us (0.86)
  Pallas kernels: 110 us -> 101 us
  local copies, waits for them, and re-layouts: 7.78 us -> 0 us
    pallas_call x1 -> x2, Pallas kernels: 110 us -> 101 us  [the longest x1 98.3 us: exchange(): pl.pallas_call(kernel, name='exchange', out_shape=(pltpu.VMEM((EXPERTS, T...]
    unnamed x7 -> x0, local copies, waits for them, and re-layouts: 7.78 us -> none
where the time goes in v3:
time: 102 us
  Pallas kernels  101 us (99%)
    pallas_call x1, Pallas kernels, exchange(): pl.pallas_call(kernel, name='exchange', out_shape=(pltpu.VMEM((EXPERTS, T...  98.3 us
    pallas_call x1, Pallas kernels, written(): pl.pallas_call(write_out, name='write_out', out_shape=tuple((jax.ShapeDty...  2.84 us

profile of v3, /device:TPU:0, one launch (start us, length us, event | category | flops | bytes accessed | tf_op | source)
XLA Modules:
  0.0 101.8 jit_solution(7172577085937119983)
XLA Ops:
  0.6 98.3 %exchange.1 = (bf16[4,25,8,4096]{3,2,1,0:T(8,128)(2,1)S(1)}, f32[4,200]{1,0:T(4,128)S(1)}, bf16[16,4096]{1,0:T(8,128)(2,1)S(1)}) custom-call(f32[4,800,8,128]{3,2,1,0:T(8,128)} %bitcast.6, bf16[4,800,8,128]{3,2,1,0:T(8,128)(2,1)} %bitcast.7, f32[4,128]{1,0:T(4,128)} %bitcast.8, f32[1,128]{1,0:T(1,128)} %bitcast.9), custom_call_target="tpu_custom_call" | custom-call | tf_op jit(solution)/shard_map/exchange/pallas_call | solution.py:414
  99.0 2.8 %write_out.1 = (bf16[4,25,8,4096]{3,2,1,0:T(8,128)(2,1)}, f32[4,200]{1,0:T(4,128)}, bf16[16,4096]{1,0:T(8,128)(2,1)}) custom-call(bf16[4,25,8,4096]{3,2,1,0:T(8,128)(2,1)S(1)} %get-tuple-element.9.final, f32[4,200]{1,0:T(4,128)S(1)} %get-tuple-element.10.scale, bf16[16,4096]{1,0:T(8,128)(2,1)S(1)} %get-tuple-element.11.serve), custom_call_target="tpu_custom_call" | custom-call | tf_op jit(solution)/shard_map/write_out/pallas_call | solution.py:472

commit v4 on v3

--- a/solution.py
+++ b/solution.py
@@ -15,13 +15,8 @@
 EXPERTS = 4
 TILES = 25
 UNROLL = 8
-SUM_GROUPS = ((0,), (1, 2, 3))
-
-
-def place_of(e):
-    g = next(i for i, group in enumerate(SUM_GROUPS) if e in group)
-    return g, SUM_GROUPS[g].index(e)
-
+
+SUM_ORDERS = ("xyz", "xyz", "yzx", "zxy")
 
 PARTS = (("xyz", 0, 9), ("yzx", 9, 8), ("zxy", 17, 8))
 
@@ -59,19 +54,14 @@
     buf0,
     buf1,
     buf2,
-    sums_out0,
-    sums_out1,
-    sums_in0,
-    sums_in1,
-    inverse0,
-    inverse1,
+    sums,
+    sums_in,
+    inverse,
     scales,
     columns,
     load_sem,
     sums_send,
     sums_recv,
-    inv_send,
-    inv_recv,
     part_send,
     part_recv,
     ep_send,
@@ -80,22 +70,20 @@
     router_recv,
 ):
     bufs = (buf0, buf1, buf2)
-    sums_out = (sums_out0, sums_out1)
-    sums_in = (sums_in0, sums_in1)
-    inverse = (inverse0, inverse1)
     me = lax.axis_index("fsdp")
     ep = lax.axis_index("ep")
     at = coords(me)
 
     barrier = pltpu.get_barrier_semaphore()
 
-    def greet(r, _):
-        pl.semaphore_signal(
-            barrier, inc=1, device_id={"fsdp": moved(at, coords(r), 1)}, device_id_type=MESH
-        )
-        return _
-
-    lax.fori_loop(1, GROUP, greet, 0)
+    for dim in "zyx":
+        for k in range(1, SIZES[dim]):
+            pl.semaphore_signal(
+                barrier,
+                inc=1,
+                device_id={"fsdp": moved(at, along(dim, k), 1)},
+                device_id_type=MESH,
+            )
     for k in range(1, 4):
         pl.semaphore_signal(
             barrier, inc=1, device_id={"ep": lax.rem(ep + k, 4)}, device_id_type=MESH
@@ -120,84 +108,72 @@
     def add_up(e):
         for copy in loads(e):
             copy.wait()
-        g, i = place_of(e)
 
         def some(step, _):
             key = places()
             packed = []
             for u in range(UNROLL):
-                value = merged_rows(e, moved(at, coords(step * UNROLL + u), 1))
-                sums = jnp.sum(value * value, axis=2, keepdims=True)
+                value = merged_rows(e, step * UNROLL + u)
+                row_sums = jnp.sum(value * value, axis=2, keepdims=True)
                 acc = jnp.zeros((8, 128), jnp.float32)
                 for j in range(TILES):
-                    acc = jnp.where(key == j, sums[j], acc)
+                    acc = jnp.where(key == j, row_sums[j], acc)
                 packed.append(acc)
             for u, acc in enumerate(packed):
-                r = step * UNROLL + u
-                sums_out[g][r, i, 0:1] = jnp.sum(acc[0:4], axis=0, keepdims=True)
-                sums_out[g][r, i, 1:2] = jnp.sum(acc[4:8], axis=0, keepdims=True)
+                for h in range(2):
+                    row = 2 * (u % 4) + h
+                    sums[e, 0, step * (UNROLL // 4) + u // 4, row : row + 1] = jnp.sum(
+                        acc[4 * h : 4 * h + 4], axis=0, keepdims=True
+                    )
             return _
 
         lax.fori_loop(0, GROUP // UNROLL, some, 0)
-
-    def sums_copy(g, r):
-        return pltpu.make_async_remote_copy(
-            src_ref=sums_out[g].at[r],
-            dst_ref=sums_in[g].at[r],
-            send_sem=sums_send.at[g],
-            recv_sem=sums_recv.at[g],
-            device_id={"fsdp": moved(at, coords(r), 1)},
-            device_id_type=MESH,
-        )
-
-    def inv_copy(g, r):
-        return pltpu.make_async_remote_copy(
-            src_ref=inverse[g].at[0],
-            dst_ref=inverse[g].at[r],
-            send_sem=inv_send.at[g],
-            recv_sem=inv_recv.at[g],
-            device_id={"fsdp": moved(at, coords(r), 1)},
-            device_id_type=MESH,
-        )
-
-    def start_all(copy, g):
-        def one(r, _):
-            copy(g, r).start()
-            return _
-
-        lax.fori_loop(1, GROUP, one, 0)
 
     def wait_bytes(ref, sem):
         pltpu.make_async_copy(ref, ref, sem).wait()
 
-    def others_of(ref):
-        return ref.at[pl.ds(1, GROUP - 1)]
-
-    def send_sums(g):
-        sums_in[g][0] = sums_out[g][0]
-        start_all(sums_copy, g)
-
-    def send_inverse(g):
-        wait_bytes(others_of(sums_in[g]), sums_recv.at[g])
-        for i, e in enumerate(SUM_GROUPS[g]):
-            root = jnp.sqrt(jnp.sum(sums_in[g][:, i], axis=0))
-            scales[e] = root
-            inverse[g][0, i] = 1.0 / root
-        start_all(inv_copy, g)
+    def arrivals(e, s):
+        sizes = [SIZES[dim] - 1 for dim in SUM_ORDERS[e]]
+        return sums_in.at[e, pl.ds(sum(sizes[:s]), sizes[s])]
+
+    def send_sums(e, s):
+        dim = SUM_ORDERS[e][s] if s < 3 else None
+        if s:
+            came = arrivals(e, s - 1)
+            wait_bytes(came, sums_recv.at[e, s - 1])
+            total = sums[e, s - 1]
+            for k in range(came.shape[0]):
+                total = total + came[k]
+            sums[e, s] = total
+        if dim is None:
+            root = jnp.sqrt(total)
+            inverse[e] = 1.0 / root
+            index = lax.broadcasted_iota(jnp.int32, root.shape, 0) * 4
+            index = index + lax.broadcasted_iota(jnp.int32, root.shape, 1) // 2
+            mine = jnp.sum(jnp.where(index == me, root, 0.0), axis=0)
+            row = lax.rem(lax.broadcasted_iota(jnp.int32, mine.shape, 0), 2)
+            for h in range(2):
+                scales[e, h : h + 1] = jnp.sum(
+                    jnp.where(row == h, mine, 0.0), axis=0, keepdims=True
+                )
+            return
+        for k in range(1, SIZES[dim]):
+            pltpu.make_async_remote_copy(
+                src_ref=sums.at[e, s],
+                dst_ref=arrivals(e, s).at[k - 1],
+                send_sem=sums_send.at[e, s],
+                recv_sem=sums_recv.at[e, s],
+                device_id={"fsdp": moved(at, along(dim, k), 1)},
+                device_id_type=MESH,
+            ).start()
 
     def normalise(e):
-        g, i = place_of(e)
-        if i == 0:
-            wait_bytes(others_of(inverse[g]), inv_recv.at[g])
-
         def some(step, _):
             key = places()
             factors = []
             for u in range(UNROLL):
-                offset = coords(step * UNROLL + u)
-                back = {dim: lax.rem(SIZES[dim] - offset[dim], SIZES[dim]) for dim in "zyx"}
-                owner = sum(back[dim] * STRIDES[dim] for dim in "zyx")
-                packed = inverse[g][owner, i]
+                row = 2 * (u % 4)
+                packed = inverse[e, step * (UNROLL // 4) + u // 4, row : row + 2]
                 spread = jnp.concatenate(
                     [jnp.broadcast_to(packed[h : h + 1], (4, 128)) for h in range(2)], axis=0
                 )
@@ -208,9 +184,10 @@
                     ]
                 )
             for u in range(UNROLL):
-                offset = coords(step * UNROLL + u)
-                value = merged_rows(e, moved(at, offset, 1)) * jnp.stack(factors[u])
-                value = value.astype(jnp.bfloat16)
+                owner = step * UNROLL + u
+                there = coords(owner)
+                offset = {dim: lax.rem(there[dim] - at[dim] + SIZES[dim], SIZES[dim]) for dim in "zyx"}
+                value = (merged_rows(e, owner) * jnp.stack(factors[u])).astype(jnp.bfloat16)
                 for buf, (order, first, count) in zip(bufs, PARTS):
                     a, b, c = order
                     one_slot = lax.rem(offset[a] + SIZES[a] - 1, SIZES[a])
@@ -232,7 +209,7 @@
                 device_id={"fsdp": moved(at, along(order[0], k), 1)},
                 device_id_type=MESH,
             )
-            for k in ((1, 3, 2) if n[0] == 4 else (1,))
+            for k in ((2, 1, 3) if n[0] == 4 else (1,))
         ]
 
     def second_copies(e, p):
@@ -247,7 +224,7 @@
                 device_id={"fsdp": moved(at, along(order[1], k), 1)},
                 device_id_type=MESH,
             )
-            for k in ((1, 3, 2) if n[1] == 4 else (1,))
+            for k in ((2, 1, 3) if n[1] == 4 else (1,))
         ]
 
     def column(order, i, j):
@@ -274,7 +251,7 @@
             ).start()
             return k
 
-        for k in (1, 3, 2) if n[2] == 4 else (1,):
+        for k in (2, 1, 3) if n[2] == 4 else (1,):
             lax.fori_loop(0, n[0] * n[1], one, k)
 
         def keep(i, _):
@@ -318,46 +295,70 @@
             device_id_type=MESH,
         )
 
-    def router_ref():
-        return serve.at[:, pl.ds(pl.multiple_of(me * 128, 128), 128)]
-
-    def router_copy(_, r):
-        return pltpu.make_async_remote_copy(
-            src_ref=router_ref(),
-            dst_ref=router_ref(),
-            send_sem=router_send,
-            recv_sem=router_recv,
-            device_id={"fsdp": moved(at, coords(r), 1)},
-            device_id_type=MESH,
-        )
-
-    def send_router():
-        for k in range(1, 4):
-            ep_copy(k).wait_recv()
-        rows = jnp.concatenate([columns[lax.rem(ep + 4 - i, 4)] for i in range(4)], axis=0)
-        serve[:, pl.ds(pl.multiple_of(me * 128, 128), 128)] = rows.astype(jnp.bfloat16)
-        start_all(router_copy, 0)
+    spans = ((me, 1, "x"), (me // 4 * 4, 4, "y"), (me // 8 * 8, 8, "z"))
+
+    def router_copies(s):
+        start, count, dim = spans[s]
+        span = serve.at[:, pl.ds(pl.multiple_of(start * 128, 128), count * 128)]
+        return [
+            pltpu.make_async_remote_copy(
+                src_ref=span,
+                dst_ref=span,
+                send_sem=router_send.at[s, k - 1],
+                recv_sem=router_recv.at[s, k - 1],
+                device_id={"fsdp": moved(at, along(dim, k), 1)},
+                device_id_type=MESH,
+            )
+            for k in range(1, SIZES[dim])
+        ]
+
+    def send_router(s):
+        if s == 0:
+            for k in range(1, 4):
+                ep_copy(k).wait_recv()
+            rows = jnp.concatenate([columns[lax.rem(ep + 4 - i, 4)] for i in range(4)], axis=0)
+            serve[:, pl.ds(pl.multiple_of(me * 128, 128), 128)] = rows.astype(jnp.bfloat16)
+        else:
+            for copy in router_copies(s - 1):
+                copy.wait_recv()
+        for copy in router_copies(s):
+            copy.start()
 
     add_up(0)
-    pl.semaphore_wait(barrier, GROUP - 1 + 3)
-    send_sums(0)
+    pl.semaphore_wait(barrier, 10)
+    send_sums(0, 0)
     for k in range(1, 4):
         ep_copy(k).start()
-    for e in SUM_GROUPS[1]:
-        add_up(e)
-    send_sums(1)
-    send_inverse(0)
-    send_router()
-    send_inverse(1)
+    add_up(1)
+    send_sums(1, 0)
+    add_up(2)
+    send_sums(2, 0)
+    send_sums(0, 1)
+    add_up(3)
+    send_sums(3, 0)
+    send_sums(1, 1)
+    send_sums(0, 2)
+    send_sums(2, 1)
+    send_sums(3, 1)
+    send_router(0)
+    send_sums(1, 2)
+    send_sums(0, 3)
     normalise(0)
+    send_sums(2, 2)
+    send_sums(3, 2)
     stage(0, 0)
+    send_sums(1, 3)
     normalise(1)
     stage(1, 0)
+    send_router(1)
     stage(0, 1)
+    send_sums(2, 3)
     normalise(2)
     stage(2, 0)
     stage(1, 1)
     stage(0, 2)
+    send_router(2)
+    send_sums(3, 3)
     normalise(3)
     stage(3, 0)
     stage(2, 1)
@@ -384,9 +385,9 @@
     stage(2, 2)
     stage(3, 2)
 
-    for g in range(len(SUM_GROUPS)):
-        wait_bytes(others_of(sums_out[g]), sums_send.at[g])
-        wait_bytes(others_of(inverse[g]), inv_send.at[g])
+    for e in range(EXPERTS):
+        for s in range(3):
+            wait_bytes(arrivals(e, s), sums_send.at[e, s])
     for e in range(EXPERTS):
         for p in range(3):
             for copy in first_copies(e, p) + second_copies(e, p):
@@ -395,9 +396,11 @@
             wait_bytes(third_bytes(e, p), part_recv.at[e, p, 2, 0])
     for k in range(1, 4):
         ep_copy(k).wait_send()
-    others = serve.at[:, pl.ds(0, (GROUP - 1) * 128)]
-    wait_bytes(others, router_send)
-    wait_bytes(others, router_recv)
+    for s in range(3):
+        for copy in router_copies(s):
+            copy.wait_send()
+            if s == 2:
+                copy.wait_recv()
 
 
 def exchange(master, second, weight, gain):
@@ -425,23 +428,20 @@
             pltpu.VMEM(rows, jnp.float32),
             pltpu.VMEM(rows, jnp.bfloat16),
             *part_bufs,
-            *(
-                pltpu.VMEM((GROUP, len(group), 2, 128), jnp.float32)
-                for group in SUM_GROUPS + SUM_GROUPS + SUM_GROUPS
-            ),
+            pltpu.VMEM((EXPERTS, 4, GROUP // 4, 8, 128), jnp.float32),
+            pltpu.VMEM((EXPERTS, 7, GROUP // 4, 8, 128), jnp.float32),
+            pltpu.VMEM((EXPERTS, GROUP // 4, 8, 128), jnp.float32),
             pltpu.VMEM((EXPERTS, 2, 128), jnp.float32),
             pltpu.VMEM((4, 4, 128), jnp.float32),
             dma((2, EXPERTS)),
-            dma((len(SUM_GROUPS),)),
-            dma((len(SUM_GROUPS),)),
-            dma((len(SUM_GROUPS),)),
-            dma((len(SUM_GROUPS),)),
+            dma((EXPERTS, 3)),
+            dma((EXPERTS, 3)),
             dma((EXPERTS, 3, 3, 3)),
             dma((EXPERTS, 3, 3, 3)),
             dma((4,)),
             dma((4,)),
-            dma(()),
-            dma(()),
+            dma((3, 3)),
+            dma((3, 3)),
         ],
         compiler_params=pltpu.CompilerParams(
             collective_id=0, has_side_effects=True, vmem_limit_bytes=48 * 2**20

time: 102 us -> 101 us (level)
  Pallas kernels: 101 us -> 99.8 us
    pallas_call x1, Pallas kernels: 98.3 us -> 97 us  [exchange(): pl.pallas_call(kernel, name='exchange', out_shape=(pltpu.VMEM((EXPERTS, T...]
where the time goes in v4:
time: 101 us; the launch traced here: 100 us
  Pallas kernels  99.8 us (99%)
    pallas_call x1, Pallas kernels, exchange(): pl.pallas_call(kernel, name='exchange', out_shape=(pltpu.VMEM((EXPERTS, T...  97 us
    pallas_call x1, Pallas kernels, written(): pl.pallas_call(write_out, name='write_out', out_shape=tuple((jax.ShapeDty...  2.84 us

profile of v4, /device:TPU:0, one launch (start us, length us, event | category | flops | bytes accessed | tf_op | source)
XLA Modules:
  0.0 100.5 jit_solution(14984938083445593913)
XLA Ops:
  0.6 97.0 %exchange.1 = (bf16[4,25,8,4096]{3,2,1,0:T(8,128)(2,1)S(1)}, f32[4,200]{1,0:T(4,128)S(1)}, bf16[16,4096]{1,0:T(8,128)(2,1)S(1)}) custom-call(f32[4,800,8,128]{3,2,1,0:T(8,128)} %bitcast.6, bf16[4,800,8,128]{3,2,1,0:T(8,128)(2,1)} %bitcast.7, f32[4,128]{1,0:T(4,128)} %bitcast.8, f32[1,128]{1,0:T(1,128)} %bitcast.9), custom_call_target="tpu_custom_call" | custom-call | tf_op jit(solution)/shard_map/exchange/pallas_call | solution.py:417
  97.6 2.8 %write_out.1 = (bf16[4,25,8,4096]{3,2,1,0:T(8,128)(2,1)}, f32[4,200]{1,0:T(4,128)}, bf16[16,4096]{1,0:T(8,128)(2,1)}) custom-call(bf16[4,25,8,4096]{3,2,1,0:T(8,128)(2,1)S(1)} %get-tuple-element.9.final, f32[4,200]{1,0:T(4,128)S(1)} %get-tuple-element.10.scale, bf16[16,4096]{1,0:T(8,128)(2,1)S(1)} %get-tuple-element.11.serve), custom_call_target="tpu_custom_call" | custom-call | tf_op jit(solution)/shard_map/write_out/pallas_call | solution.py:472

commit v5 on v4

--- a/solution.py
+++ b/solution.py
@@ -14,7 +14,7 @@
 GROUP = 32
 EXPERTS = 4
 TILES = 25
-UNROLL = 8
+UNROLL = 16
 
 SUM_ORDERS = ("xyz", "xyz", "yzx", "zxy")
 
@@ -344,9 +344,9 @@
     send_sums(1, 2)
     send_sums(0, 3)
     normalise(0)
+    stage(0, 0)
     send_sums(2, 2)
     send_sums(3, 2)
-    stage(0, 0)
     send_sums(1, 3)
     normalise(1)
     stage(1, 0)
@@ -364,6 +364,10 @@
     stage(2, 1)
     stage(1, 2)
 
+    stage(3, 1)
+    stage(2, 2)
+    stage(3, 2)
+
     def order_of(index):
         source = lax.broadcasted_iota(jnp.int32, (128, 256), 0)
         target = lax.broadcasted_iota(jnp.int32, (128, 256), 1)
@@ -380,10 +384,6 @@
         for index in range(2)
     )
     scale[...] = in_rows[:, 0 : TILES * 8]
-
-    stage(3, 1)
-    stage(2, 2)
-    stage(3, 2)
 
     for e in range(EXPERTS):
         for s in range(3):

time: 101 us -> 100 us (0.990)
  no operation moved by 1% of the time
where the time goes in v5:
time: 100 us
  Pallas kernels  99.5 us (100%)
    pallas_call x1, Pallas kernels, exchange(): pl.pallas_call(kernel, name='exchange', out_shape=(pltpu.VMEM((EXPERTS, T...  96.6 us
    pallas_call x1, Pallas kernels, written(): pl.pallas_call(write_out, name='write_out', out_shape=tuple((jax.ShapeDty...  2.84 us

profile of v5, /device:TPU:0, one launch (start us, length us, event | category | flops | bytes accessed | tf_op | source)
XLA Modules:
  0.0 100.1 jit_solution(7597150823774795633)
XLA Ops:
  0.6 96.6 %exchange.1 = (bf16[4,25,8,4096]{3,2,1,0:T(8,128)(2,1)S(1)}, f32[4,200]{1,0:T(4,128)S(1)}, bf16[16,4096]{1,0:T(8,128)(2,1)S(1)}) custom-call(f32[4,800,8,128]{3,2,1,0:T(8,128)} %bitcast.6, bf16[4,800,8,128]{3,2,1,0:T(8,128)(2,1)} %bitcast.7, f32[4,128]{1,0:T(4,128)} %bitcast.8, f32[1,128]{1,0:T(1,128)} %bitcast.9), custom_call_target="tpu_custom_call" | custom-call | tf_op jit(solution)/shard_map/exchange/pallas_call | solution.py:417
  97.3 2.8 %write_out.1 = (bf16[4,25,8,4096]{3,2,1,0:T(8,128)(2,1)}, f32[4,200]{1,0:T(4,128)}, bf16[16,4096]{1,0:T(8,128)(2,1)}) custom-call(bf16[4,25,8,4096]{3,2,1,0:T(8,128)(2,1)S(1)} %get-tuple-element.9.final, f32[4,200]{1,0:T(4,128)S(1)} %get-tuple-element.10.scale, bf16[16,4096]{1,0:T(8,128)(2,1)S(1)} %get-tuple-element.11.serve), custom_call_target="tpu_custom_call" | custom-call | tf_op jit(solution)/shard_map/write_out/pallas_call | solution.py:472

commit v6 on v5

--- a/solution.py
+++ b/solution.py
@@ -18,7 +18,7 @@
 
 SUM_ORDERS = ("xyz", "xyz", "yzx", "zxy")
 
-PARTS = (("xyz", 0, 9), ("yzx", 9, 8), ("zxy", 17, 8))
+PARTS = (("xyz", 0, 8), ("yzx", 8, 8), ("zxy", 16, 9))
 
 
 def coords(index):
@@ -456,10 +456,16 @@
 
 def write_out(final, scale, serve, final_out, scale_out, serve_out, sem):
     copies = [
-        pltpu.make_async_copy(final.at[e], final_out.at[e], sem.at[e]) for e in range(EXPERTS)
+        pltpu.make_async_copy(serve, serve_out, sem.at[2 * EXPERTS]),
+        pltpu.make_async_copy(scale, scale_out, sem.at[2 * EXPERTS + 1]),
     ]
-    copies.append(pltpu.make_async_copy(serve, serve_out, sem.at[EXPERTS]))
-    copies.append(pltpu.make_async_copy(scale, scale_out, sem.at[EXPERTS + 1]))
+    for e in range(EXPERTS):
+        for h, tiles in enumerate((pl.ds(0, 13), pl.ds(13, 12))):
+            copies.append(
+                pltpu.make_async_copy(
+                    final.at[e, tiles], final_out.at[e, tiles], sem.at[2 * e + h]
+                )
+            )
     for copy in copies:
         copy.start()
     for copy in copies:
@@ -477,7 +483,7 @@
         ),
         in_specs=[vmem] * 3,
         out_specs=(hbm,) * 3,
-        scratch_shapes=[pltpu.SemaphoreType.DMA((EXPERTS + 2,))],
+        scratch_shapes=[pltpu.SemaphoreType.DMA((2 * EXPERTS + 2,))],
         compiler_params=pltpu.CompilerParams(vmem_limit_bytes=16 * 2**20),
     )(final, scale, serve)
 

time: 100 us -> 100 us (level)
  no operation moved by 1% of the time
where the time goes in v6:
time: 100 us
  Pallas kernels  99.5 us (100%)
    pallas_call x1, Pallas kernels, exchange(): pl.pallas_call(kernel, name='exchange', out_shape=(pltpu.VMEM((EXPERTS, T...  96.6 us
    pallas_call x1, Pallas kernels, written(): pl.pallas_call(write_out, name='write_out', out_shape=tuple((jax.ShapeDty...  2.87 us

profile of v6, /device:TPU:0, one launch (start us, length us, event | category | flops | bytes accessed | tf_op | source)
XLA Modules:
  0.0 100.2 jit_solution(12495772052519440636)
XLA Ops:
  0.6 96.6 %exchange.1 = (bf16[4,25,8,4096]{3,2,1,0:T(8,128)(2,1)S(1)}, f32[4,200]{1,0:T(4,128)S(1)}, bf16[16,4096]{1,0:T(8,128)(2,1)S(1)}) custom-call(f32[4,800,8,128]{3,2,1,0:T(8,128)} %bitcast.6, bf16[4,800,8,128]{3,2,1,0:T(8,128)(2,1)} %bitcast.7, f32[4,128]{1,0:T(4,128)} %bitcast.8, f32[1,128]{1,0:T(1,128)} %bitcast.9), custom_call_target="tpu_custom_call" | custom-call | tf_op jit(solution)/shard_map/exchange/pallas_call | solution.py:417
  97.3 2.9 %write_out.1 = (bf16[4,25,8,4096]{3,2,1,0:T(8,128)(2,1)}, f32[4,200]{1,0:T(4,128)}, bf16[16,4096]{1,0:T(8,128)(2,1)}) custom-call(bf16[4,25,8,4096]{3,2,1,0:T(8,128)(2,1)S(1)} %get-tuple-element.9.final, f32[4,200]{1,0:T(4,128)S(1)} %get-tuple-element.10.scale, bf16[16,4096]{1,0:T(8,128)(2,1)S(1)} %get-tuple-element.11.serve), custom_call_target="tpu_custom_call" | custom-call | tf_op jit(solution)/shard_map/write_out/pallas_call | solution.py:478
